TPU v7x, 128 devices: a whole 4x4x4 slice. The times are simulated.
128 devices in a mesh: ctx: 8 (over z_hi, x), tp: 8 (over y, core), ep: 2 (over z_lo).
Axes of the slice: x: 4, y: 4, z: 4 (z_hi: 2, z_lo: 2; z = z_hi * 2 + z_lo), core: 2. Of those that a mesh axis runs over, the one named last changes fastest.
Arguments:
- resid: bfloat16 [2048, 6144], P('ctx', ('tp', 'ep')), may hold values from -60 to 60
- queries: bfloat16 [2048, 6144], P('ctx', 'tp'), may hold values from -6 to 6
- keys: bfloat16 [2048, 1024], P('ctx', 'tp'), may hold values from -4 to 4
- values: bfloat16 [2048, 1024], P('ctx', 'tp'), may hold values from -5 to 5
- w_out: bfloat16 [6144, 6144], P('tp', ('ctx', 'ep')), may hold values from -0.078125 to 0.078125
- norm_gain: bfloat16 [6144], P(('tp', 'ep')), may hold values from 0.5 to 1.5
- w_gate: bfloat16 [8, 6144, 8192], P('tp', None, ('ctx', 'ep')), may hold values from -0.078125 to 0.078125
- w_up: bfloat16 [8, 6144, 8192], P('tp', None, ('ctx', 'ep')), may hold values from -0.078125 to 0.078125
- w_down: bfloat16 [8, 8192, 6144], P('tp', ('ctx', 'ep')), may hold values from -0.0625 to 0.0625
- expert_ids: int32 [2048, 2], P('ctx'), may hold values from 0 to 7, all different within a row; in each aligned block of 256 rows (0 to 255, 256 to 511, ...) at most 96 rows name the same one
- route_units: int32 [2048, 2], P('ctx'), may hold values from 1 to 65535
Outputs:
- mixed: bfloat16 [2048, 6144], P('ctx', ('tp', 'ep'))
Inputs may be any that keep to these rules, and one draw needn't show every extreme that they name: `expert_ids`: each row names two different experts; in every aligned block of 256 rows no expert is named by more than 96 rows, a bound that some block reaches.
All inputs are finite; a program needn't handle non-finite values.
Results may differ from a plain program's by a relative error of at most 0.01.
Values may be sent and summed in bfloat16 or wider, within the bound.
A program may use at most 128 MiB of HBM per device.

v0:
```python
import jax
import jax.numpy as jnp
from jax import lax
from jax.sharding import Mesh
from jax.sharding import PartitionSpec as P

D = 6144
HD = 128
TP = ("tp_0", "tp_1")
TP_EP = ("tp_0", "tp_1", "ep")


def split_up(x, dim, size):
    dims = x.shape
    tiles = x.reshape(*dims[:dim], size, dims[dim] // size, *dims[dim + 1 :])
    return jnp.moveaxis(tiles, dim, 0)


def sent_and_summed(x, axis, dim):
    tiles = split_up(x, dim, lax.axis_size(axis))
    arrived = lax.all_to_all(tiles, axis, split_axis=0, concat_axis=0, tiled=True)
    return arrived.astype(jnp.float32).sum(axis=0)


def from_everyone(x, axis):
    size = lax.axis_size(axis)
    return lax.all_to_all(jnp.broadcast_to(x[None], (size, *x.shape)), axis, 0, 0, tiled=True)


def taken_together(x, axis):
    everything = from_everyone(x, axis)
    return jnp.sum(everything, axis=0)


def laid_out(tiles, dim):
    dims = list(tiles.shape[1:])
    dims[dim] *= tiles.shape[0]
    return jnp.moveaxis(tiles, 0, dim).reshape(dims)


def moved_by_axis(tiles, axes, sequence):
    dims = [lax.axis_size(a) for a in axes]
    tiles = tiles.reshape(*dims, *tiles.shape[1:])
    for k in sequence:
        tiles = lax.all_to_all(tiles, axes[k], split_axis=k, concat_axis=k, tiled=True)
    return tiles.reshape(-1, *tiles.shape[len(axes) :])


def one_axis_at_a_time(x, axes, sequence, split_dim, concat_dim):
    tiles = split_up(x, split_dim, lax.axis_size(axes))
    return laid_out(moved_by_axis(tiles, axes, sequence), concat_dim)


def from_partner(x, axis, distance):
    return lax.ppermute(x, axis, [(i, i ^ 1 << distance) for i in range(lax.axis_size(axis))])


def on_device(
    resid, queries, keys, values, w_out, norm_gain, w_gate, w_up, w_down, expert_ids, route_units
):
    tp_size = lax.axis_size(TP)
    ep_size = lax.axis_size("ep")
    ctx_size = lax.axis_size("ctx")
    tok_rows = queries.shape[0]
    heads_dev = queries.shape[1] // HD
    kv_dev = keys.shape[1] // HD
    group = heads_dev // kv_dev
    feat_dev = resid.shape[1]
    hidden_dev = w_gate.shape[2]
    capacity = 3 * tok_rows // tp_size
    first_pos = lax.axis_index("ctx") * tok_rows
    query_heads = queries.reshape(tok_rows, kv_dev, group, HD)
    query_pos = first_pos + jnp.arange(tok_rows, dtype=jnp.int32)
    running_max = jnp.full((kv_dev, group, tok_rows), -1e30, jnp.float32)
    key_piece = lax.all_gather(keys, "ctx", axis=0, tiled=True)
    value_piece = lax.all_gather(values, "ctx", axis=0, tiled=True)
    count = key_piece.shape[0]
    key_rows = key_piece.reshape(count, kv_dev, HD)
    value_rows = value_piece.reshape(count, kv_dev, HD)
    scores = jnp.einsum(
        "tkgd,nkd->kgtn", query_heads, key_rows, preferred_element_type=jnp.float32
    ) * HD ** (-0.5)
    key_pos = jnp.arange(count, dtype=jnp.int32)
    allowed = (key_pos[None, :] <= query_pos[:, None])[None, None]
    block_max = jnp.max(jnp.where(allowed, scores, -1e30), axis=-1)
    new_max = jnp.maximum(running_max, block_max)
    probs = jnp.where(allowed, jnp.exp(scores - new_max[..., None]), 0.0)
    new_sum = jnp.sum(probs, axis=-1)
    probs_b = probs.astype(jnp.bfloat16)
    update = jnp.einsum("kgtn,nkd->kgtd", probs_b, value_rows, preferred_element_type=jnp.float32)
    attn = (
        (update / new_sum[..., None])
        .transpose(2, 0, 1, 3)
        .reshape(tok_rows, heads_dev * HD)
        .astype(jnp.bfloat16)
    )
    partial_proj = jnp.dot(
        attn, lax.all_gather(w_out, "ctx", axis=1, tiled=True), preferred_element_type=jnp.float32
    )
    proj = sent_and_summed(partial_proj.astype(jnp.bfloat16), TP, 1)
    hres = (resid.astype(jnp.float32) + proj).astype(jnp.bfloat16)
    hfloat = hres.astype(jnp.float32)
    square_total = taken_together(jnp.sum(hfloat * hfloat, axis=1, keepdims=True), TP_EP)
    normed = (hfloat * lax.rsqrt(square_total / D + 1e-05) * norm_gain.astype(jnp.float32)).astype(
        jnp.bfloat16
    )
    onehot = (expert_ids[..., None] == jnp.arange(tp_size, dtype=jnp.int32)).astype(jnp.int32)
    per_token = jnp.sum(onehot, axis=1)
    earlier = jnp.cumsum(per_token, axis=0) - per_token
    slot = jnp.sum(onehot * earlier[:, None, :], axis=-1)
    codes = expert_ids * capacity + slot
    slot_ids = jnp.arange(tp_size * capacity, dtype=jnp.int32)
    picks = (
        (slot_ids[:, None] == codes[None, :, 0]) | (slot_ids[:, None] == codes[None, :, 1])
    ).astype(jnp.bfloat16)
    dispatched = jnp.dot(picks, normed, preferred_element_type=jnp.float32).astype(jnp.bfloat16)
    dispatched = dispatched.reshape(tp_size, 1, capacity, feat_dev)
    arrived = one_axis_at_a_time(dispatched, TP, (1, 0), 0, 1)
    gate_w = w_gate[0].reshape(tp_size, ep_size, feat_dev, hidden_dev)
    up_w = w_up[0].reshape(tp_size, ep_size, feat_dev, hidden_dev)
    zero_acc = jnp.zeros((ctx_size, capacity, hidden_dev), jnp.float32)
    piece = lax.all_gather(arrived, ("ctx", "ep"), axis=0, tiled=True)

    def one_row(index, totals):
        gate_total, up_total = totals
        source = index // ep_size
        parity = index % ep_size
        row = lax.dynamic_index_in_dim(piece, index, 0, keepdims=False)
        gate_part = lax.dynamic_index_in_dim(gate_w, parity, 1, keepdims=False)
        up_part = lax.dynamic_index_in_dim(up_w, parity, 1, keepdims=False)
        gate_add = jnp.einsum("tsj,tjf->sf", row, gate_part, preferred_element_type=jnp.float32)
        up_add = jnp.einsum("tsj,tjf->sf", row, up_part, preferred_element_type=jnp.float32)
        gate_now = lax.dynamic_index_in_dim(gate_total, source, 0, keepdims=False) + gate_add
        up_now = lax.dynamic_index_in_dim(up_total, source, 0, keepdims=False) + up_add
        return (
            lax.dynamic_update_index_in_dim(gate_total, gate_now, source, 0),
            lax.dynamic_update_index_in_dim(up_total, up_now, source, 0),
        )

    gate_acc, up_acc = lax.fori_loop(0, piece.shape[0], one_row, (zero_acc, zero_acc))
    hidden = (jax.nn.silu(gate_acc) * up_acc).astype(jnp.bfloat16)
    down_w = w_down[0].reshape(hidden_dev, tp_size, ep_size, feat_dev)
    parity = lax.axis_index("ep")
    mine_cols = lax.dynamic_index_in_dim(down_w, parity, 2, keepdims=False)
    give_cols = lax.dynamic_index_in_dim(down_w, 1 - parity, 2, keepdims=False)
    got_hidden, got_cols = from_partner((hidden, give_cols), "ep", 0)
    hidden_both = jnp.concatenate([hidden, got_hidden], axis=2)
    cols_both = jnp.concatenate([mine_cols, got_cols], axis=0)
    blocks = lax.axis_size("ctx") * capacity // capacity
    product = jnp.einsum(
        "csf,ftj->cstj", hidden_both, cols_both, preferred_element_type=jnp.float32
    )
    expert_sum = lax.psum_scatter(
        product.reshape(blocks * capacity, tp_size * feat_dev).astype(jnp.bfloat16),
        "ctx",
        scatter_dimension=0,
        tiled=True,
    )
    expert_out = expert_sum.reshape(1, capacity, tp_size, feat_dev)
    returned = lax.all_to_all(expert_out, TP, split_axis=2, concat_axis=0, tiled=True)
    units = route_units.astype(jnp.float32)
    weights = (units / jnp.sum(units, axis=-1, keepdims=True)).astype(jnp.bfloat16)
    combine = jnp.where(slot_ids[None, :] == codes[:, 0:1], weights[:, 0:1], 0.0) + jnp.where(
        slot_ids[None, :] == codes[:, 1:2], weights[:, 1:2], 0.0
    )
    moe = jnp.dot(
        combine, returned.reshape(tp_size * capacity, feat_dev), preferred_element_type=jnp.float32
    )
    return (hfloat + moe).astype(jnp.bfloat16)


def solution(mesh):
    torus = Mesh(
        mesh.devices.reshape(mesh.shape["ctx"], 4, 2, mesh.shape["ep"]),
        ("ctx", "tp_0", "tp_1", "ep"),
    )
    in_specs = (
        P("ctx", TP_EP),
        P("ctx", TP),
        P("ctx", TP),
        P("ctx", TP),
        P(TP, ("ctx", "ep")),
        P(TP_EP),
        P(TP, None, ("ctx", "ep")),
        P(TP, None, ("ctx", "ep")),
        P(TP, ("ctx", "ep"), None),
        P("ctx", None),
        P("ctx", None),
    )
    out_specs = P("ctx", TP_EP)
    return jax.shard_map(
        on_device, mesh=torus, in_specs=in_specs, out_specs=out_specs, check_vma=False
    )
```

profile of v0, /device:TPU:1, one launch (start us, length us, event | category | flops | bytes accessed | tf_op | source)
XLA Modules:
  0.0 661.8 jit_solution(15073614211163878347)
XLA Ops:
  9.4 31.8 %all_gather.12 = bf16[2048,128]{1,0:T(8,128)(2,1)S(1)} all-gather(bf16[256,128]{1,0:T(8,128)(2,1)} %param.15), channel_id=1, replica_groups=mesh['ctx'=8,'tp_0'=4,'tp_1'=2,'ep'=2] {'ctx'}, dimensions={0}, use_global_device_ids=true | all-gather | bytes 589824 | tf_op jit(solution)/shard_map/all_gather | solution.py:75
  43.6 30.6 %all_gather.13 = bf16[2048,128]{0,1:T(8,128)(2,1)S(1)} all-gather(bf16[256,128]{0,1:T(8,128)(2,1)S(1)} %copy.47), channel_id=1, replica_groups=mesh['ctx'=8,'tp_0'=4,'tp_1'=2,'ep'=2] {'ctx'}, dimensions={0}, use_global_device_ids=true | all-gather | bytes 589824 | tf_op jit(solution)/shard_map/all_gather | solution.py:76
  76.9 2.9 fusion.55
  79.8 19.2 %all-gather.3.cloned.1.call-done = bf16[768,3072]{1,0:T(8,128)(2,1)} async-done(((bf16[768,384]{1,0:T(8,128)(2,1)}), bf16[768,3072]{1,0:T(8,128)(2,1)}) %all-gather.3.cloned.1.call-update) | async-done | bytes 4718608 | tf_op jit(solution)/shard_map/all_gather | solution.py:98
  99.0 3.8 convolution_convert_fusion
  104.1 5.7 all-to-all-start
  110.7 19.6 %all-to-all-done = bf16[8,256,384]{2,1,0:T(8,128)(2,1)S(1)} async-done(((bf16[8,256,384]{2,1,0:T(8,128)(2,1)}), bf16[8,256,384]{2,1,0:T(8,128)(2,1)S(1)}, u32[]{:S(2)}, u32[]{:S(2)}) %all-to-all-start) | async-done | bytes 1572896 | tf_op jit(solution)/shard_map/all_to_all | solution.py:21
  131.4 4.3 all-to-all-start.1
  135.7 5.8 all-to-all-done.1
  142.2 4.2 all_to_all.35
  146.4 12.7 %all_to_all.36 = bf16[4,2,1,1,96,384]{5,4,1,3,2,0:T(8,128)(2,1)} all-to-all(bf16[4,2,1,1,96,384]{5,4,1,3,2,0:T(8,128)(2,1)S(1)} %copy.51), channel_id=1, replica_groups=mesh['ctx'=8,'tp_0'=4,'tp_1'=2,'ep'=2] {'tp_0'}, dimensions={0} | all-to-all | bytes 1179648 | tf_op jit(solution)/shard_map/all_to_all | solution.py:45
  159.4 14.6 %reshape_squeeze.11 = bf16[512,8,2,384]{3,2,1,0:T(2,128)(2,1)} reshape(bf16[1,512,6144]{2,1,0:T(8,128)(2,1)} %param.21) | data formatting | bytes 12582912 | tf_op jit(solution)/shard_map/reshape;squeeze | solution.py:142
  174.0 15.4 %constant_dynamic-slice_fusion.3 = (bf16[512,8,1,384]{3,2,1,0:T(2,128)(2,1)}, bf16[512,8,1,384]{3,2,1,0:T(2,128)(2,1)S(1)}) fusion(bf16[512,8,2,384]{3,2,1,0:T(2,128)(2,1)} %reshape_squeeze.11, s32[]{:T(128)S(6)} %select_n.93, s32[]{:T(128)S(6)} %select_n.94), kind=kLoop, calls=%fused_computation.93 | loop fusion | bytes 12582920 | tf_op jit(solution)/shard_map/jit(dynamic_index_in_dim)/dynamic_slice | solution.py:144
  189.4 2.8 copy.71
  192.5 226.1 %all-gather.5.cloned.1.call-done = bf16[16,8,96,384]{3,2,1,0:T(8,128)(2,1)} async-done(((bf16[1,8,96,384]{3,2,1,0:T(8,128)(2,1)}), bf16[16,8,96,384]{3,2,1,0:T(8,128)(2,1)}) %all-gather.5.cloned.1.call-update) | async-done | bytes 9437200 | tf_op jit(solution)/shard_map/all_gather | solution.py:122
  419.0 88.4 %while.17 = (s32[]{:T(128)}, f32[8,96,512]{2,1,0:T(8,128)S(1)}, f32[8,96,512]{2,1,0:T(8,128)S(1)}, bf16[16,8,96,384]{3,2,1,0:T(8,128)(2,1)}, bf16[8,2,384,512]{3...) while((s32[]{:T(128)}, f32[8,96,512]{2,1,0:T(8,128)S(1)}, ...), condition=%wide.region_11.12_spmd, body=%wide.region_10.11_spmd.sunk | while | flops 604078080 | bytes 9045304 | solution.py:140
  419.1 2.7 fusion.102
  421.8 2.7 fusion.101
  427.3 2.7 fusion.101
  430.1 2.7 fusion.102
  432.8 2.7 fusion.101
  435.6 2.7 fusion.102
  438.4 2.7 fusion.101
  441.2 2.7 fusion.102
  443.9 2.7 fusion.101
  446.7 2.7 fusion.102
  449.4 2.7 fusion.101
  452.2 2.7 fusion.102
  454.9 2.7 fusion.101
  457.7 2.7 fusion.102
  460.5 2.7 fusion.101
  463.3 2.7 fusion.102
  466.0 2.7 fusion.101
  471.5 2.7 fusion.101
  477.0 2.7 fusion.101
  482.5 2.7 fusion.101
  488.1 2.7 fusion.101
  493.6 2.7 fusion.101
  499.1 2.7 fusion.101
  504.6 2.7 fusion.101
  507.8 7.8 %collective-permute-start = (bf16[8,96,512]{2,1,0:T(8,128)(2,1)S(1)}, bf16[8,96,512]{2,1,0:T(8,128)(2,1)S(1)}, u32[]{:S(2)}, u32[]{:S(2)}) collective-permute-start(bf16[8,96,512]{2,1,0:T(8,128)(2,1)S(1)} %multiply_convert_fusion), channel_id=1, source_target_pairs={{0,1},{1,0},{2,3},{3,2},{4,5},{5,4},{6,7},{7,6},{8,9},{9,8},{10,11... | collective-permute-start | bytes 2359304 | tf_op jit(solution)/shard_map/ppermute | solution.py:55
  515.6 3.9 copy.72
  519.5 13.0 %collective-permute-done = bf16[8,96,512]{2,1,0:T(8,128)(2,1)S(1)} collective-permute-done((bf16[8,96,512]{2,1,0:T(8,128)(2,1)S(1)}, bf16[8,96,512]{2,1,0:T(8,128)(2,1)S(1)}, u32[]{:S(2)}, u32[]{:S(2)}) %collective-permute-start) | collective-permute-done | bytes 786464 | tf_op jit(solution)/shard_map/ppermute | solution.py:55
  532.6 6.7 %fusion.48 = bf16[8,96,8,384]{3,1,2,0:T(8,128)(2,1)S(1)} fusion(bf16[512,8,384]{2,0,1:T(8,128)(2,1)} %collective-permute-done.1, bf16[512,8,384]{2,0,1:T(8,128)(2,1)S(1)} %bitcast.178, bf16[8,96,512]{2,1,0:T(8,128)(2,1)S(1)} %collective-permute-done, bf16[8,96,512]{2,1,0:T(8,128)(2,1)S(1)} %multiply_convert_fusion), kind=kOutput, calls=%fused_computation.40 | convolution fusion | flops 4849926144 | bytes 12582912 | tf_op jit(solution)/shard_map/csf,ftj->cstj/dot_general | solution.py:150
  541.1 3.3 copy.66
  544.5 91.3 %reduce-scatter.2.cloned.1.call-done = bf16[96,3072]{1,0:T(8,128)(2,1)} async-done(((bf16[768,3072]{1,0:T(8,128)(2,1)}), bf16[96,3072]{1,0:T(8,128)(2,1)}) %reduce-scatter.2.cloned.1.call-update) | async-done | bytes 589840 | tf_op jit(solution)/shard_map/reduce_scatter | solution.py:153
  637.8 6.2 all-to-all-start.4
  644.1 10.0 %all-to-all-done.4 = bf16[1,96,8,384]{3,1,0,2:T(8,128)(2,1)S(1)} async-done(((bf16[1,96,8,384]{3,1,0,2:T(8,128)(2,1)}), bf16[1,96,8,384]{3,1,0,2:T(8,128)(2,1)S(1)}, u32[]{:S(2)}, u32[]{:S(2)}) %all-to-all-start.4) | async-done | bytes 589856 | tf_op jit(solution)/shard_map/all_to_all | solution.py:160
  (80 shorter events, 40.6 us)
Async XLA Ops:
  6.5 92.4 %all-gather.3.cloned.1.call-start = ((), (), s32[]{:S(2)}) async-start(), calls=%async_computation.6 | async-start | bytes 5308416 | tf_op jit(solution)/shard_map/all_gather | solution.py:98
  102.7 7.1 %copy-start.3 = (s32[256,2]{0,1:T(2,128)S(1)}, s32[256,2]{0,1:T(2,128)}, u32[]{:S(2)}) copy-start(s32[256,2]{0,1:T(2,128)} %param.22) | copy-start | bytes 6148
  102.7 27.8 %copy-start = (bf16[256,384]{1,0:T(8,128)(2,1)S(1)}, bf16[256,384]{1,0:T(8,128)(2,1)}, u32[]{:S(2)}) copy-start(bf16[256,384]{1,0:T(8,128)(2,1)} %param.13) | copy-start | bytes 589828
  102.7 33.0 %copy-start.5 = (bf16[384]{0:T(512)(128)(2,1)S(1)}, bf16[384]{0:T(512)(128)(2,1)}, u32[]{:S(2)}) copy-start(bf16[384]{0:T(512)(128)(2,1)} %param.18) | copy-start | bytes 2308
  104.1 26.3 %all-to-all-start = ((bf16[8,256,384]{2,1,0:T(8,128)(2,1)}), bf16[8,256,384]{2,1,0:T(8,128)(2,1)S(1)}, u32[]{:S(2)}, u32[]{:S(2)}) async-start(bf16[8,256,384]{2,1,0:T(8,128)(2,1)} %bitcast.152), calls=%async_computation | async-start | bytes 3145728 | tf_op jit(solution)/shard_map/all_to_all | solution.py:21
  130.7 43.3 %copy-start.1 = (bf16[256,384]{1,0:T(8,128)(2,1)}, bf16[256,384]{1,0:T(8,128)(2,1)S(1)}, u32[]{:S(2)}) copy-start(bf16[256,384]{1,0:T(8,128)(2,1)S(1)} %get-tuple-element.198) | copy-start | bytes 589828
  131.4 10.2 %all-to-all-start.1 = ((f32[16,256,1]{1,2,0:T(1,128)}), f32[16,256,1]{1,2,0:T(1,128)S(1)}, u32[]{:S(2)}, u32[]{:S(2)}) async-start(f32[16,256,1]{1,2,0:T(1,128)} %broadcast_in_dim.96), calls=%async_computation.1 | async-start | bytes 32768 | tf_op jit(solution)/shard_map/all_to_all | solution.py:27
  135.7 282.9 %all-gather.5.cloned.1.call-start = ((), (), s32[]{:S(2)}) async-start(), calls=%async_computation.7 | async-start | bytes 10027008 | tf_op jit(solution)/shard_map/all_gather | solution.py:122
  159.2 476.6 %reduce-scatter.2.cloned.1.call-start = ((), (), s32[]{:S(2)}) async-start(), calls=%async_computation.8 | async-start | bytes 5308416 | tf_op jit(solution)/shard_map/reduce_scatter | solution.py:153
  192.2 327.3 %collective-permute-start.1 = (bf16[512,8,384]{2,0,1:T(8,128)(2,1)}, bf16[512,8,384]{2,0,1:T(8,128)(2,1)}, u32[]{:S(2)}, u32[]{:S(2)}) collective-permute-start(bf16[512,8,384]{2,0,1:T(8,128)(2,1)} %bitcast.149), channel_id=1, source_target_pairs={{0,1},{1,0},{2,3},{3,2},{4,5},{5,4},{6,7},{7,6},{8,9},{9,8},{10,11... | collective-permute-start | bytes 9437192 | tf_op jit(solution)/shard_map/ppermute | solution.py:55
  507.8 24.7 %collective-permute-start = (bf16[8,96,512]{2,1,0:T(8,128)(2,1)S(1)}, bf16[8,96,512]{2,1,0:T(8,128)(2,1)S(1)}, u32[]{:S(2)}, u32[]{:S(2)}) collective-permute-start(bf16[8,96,512]{2,1,0:T(8,128)(2,1)S(1)} %multiply_convert_fusion), channel_id=1, source_target_pairs={{0,1},{1,0},{2,3},{3,2},{4,5},{5,4},{6,7},{7,6},{8,9},{9,8},{10,11... | collective-permute-start | bytes 2359304 | tf_op jit(solution)/shard_map/ppermute | solution.py:55
  544.4 99.6 %copy-start.4 = (s32[256,2]{0,1:T(2,128)S(1)}, s32[256,2]{0,1:T(2,128)}, u32[]{:S(2)}) copy-start(s32[256,2]{0,1:T(2,128)} %param.23) | copy-start | bytes 6148
  544.4 109.6 %copy-start.2 = (bf16[256,384]{1,0:T(8,128)(2,1)S(1)}, bf16[256,384]{1,0:T(8,128)(2,1)}, u32[]{:S(2)}) copy-start(bf16[256,384]{1,0:T(8,128)(2,1)} %copy-done.1) | copy-start | bytes 589828
  637.8 16.3 %all-to-all-start.4 = ((bf16[1,96,8,384]{3,1,0,2:T(8,128)(2,1)}), bf16[1,96,8,384]{3,1,0,2:T(8,128)(2,1)S(1)}, u32[]{:S(2)}, u32[]{:S(2)}) async-start(bf16[1,96,8,384]{3,1,0,2:T(8,128)(2,1)} %copy.57), calls=%async_computation.5 | async-start | bytes 1179648 | tf_op jit(solution)/shard_map/all_to_all | solution.py:160
Sparse Core Ops, SparseCore 0:
  9.5 89.3 all-gather.2
  159.3 259.2 all-gather.4
  544.6 91.1 reduce-scatter.1
where the time goes:
time: 663 us; the launch traced here: 662 us
  waiting for transfers between devices  386 us (58%)
  matrix products  104 us (16%)
  blocking collectives  79.4 us (12%)
  local copies, waits for them, and re-layouts  49.3 us (7%)
  starting transfers between devices  24.5 us (4%)
  between operations  13.4 us (2%)
    all_gather x1, waiting for transfers between devices, on_device(): piece = lax.all_gather(arrived, ('ctx', 'ep'), axis=0, tiled=True)  226 us
    reduce_scatter x1, waiting for transfers between devices, on_device(): lax.psum_scatter(product.reshape(blocks * capacity, tp_size * feat_dev).a...  91.3 us
    dot_general x16, matrix products, one_row(): jnp.einsum('tsj,tjf->sf', row, gate_part, preferred_element_type=jnp.floa...  43.6 us
    dot_general x16, matrix products, one_row(): jnp.einsum('tsj,tjf->sf', row, up_part, preferred_element_type=jnp.float32)  43.5 us
    all_gather x1, blocking collectives, on_device(): key_piece = lax.all_gather(keys, 'ctx', axis=0, tiled=True)  31.8 us
    all_gather x1, blocking collectives, on_device(): value_piece = lax.all_gather(values, 'ctx', axis=0, tiled=True)  30.6 us
    all_to_all x1, waiting for transfers between devices, sent_and_summed(): lax.all_to_all(tiles, axis, split_axis=0, concat_axis=0, tiled=True)  19.6 us
    all_gather x1, waiting for transfers between devices, on_device(): lax.all_gather(w_out, 'ctx', axis=1, tiled=True)  19.2 us
  transfers between devices with their start and end apart: 8, of which 7 were waited for; matrix products, arithmetic and copies ran while one was open for 21% of the time, Pallas kernels for 0%

commit v1 on v0

--- a/solution.py
+++ b/solution.py
@@ -3,6 +3,7 @@
 from jax import lax
 from jax.sharding import Mesh
 from jax.sharding import PartitionSpec as P
+from jax.lax import all_to_all, axis_size
 
 D = 6144
 HD = 128
@@ -119,7 +120,15 @@
     gate_w = w_gate[0].reshape(tp_size, ep_size, feat_dev, hidden_dev)
     up_w = w_up[0].reshape(tp_size, ep_size, feat_dev, hidden_dev)
     zero_acc = jnp.zeros((ctx_size, capacity, hidden_dev), jnp.float32)
-    piece = lax.all_gather(arrived, ("ctx", "ep"), axis=0, tiled=True)
+    piece = jnp.concatenate(
+        all_to_all(
+            jnp.stack([arrived for _ in range(axis_size(("ctx", "ep")))], axis=0),
+            ("ctx", "ep"),
+            0,
+            0,
+        ),
+        axis=0,
+    )
 
     def one_row(index, totals):
         gate_total, up_total = totals

time: 663 us -> 538 us (0.81)
  waiting for transfers between devices: 386 us -> 257 us
    all_gather x1 -> x0, waiting for transfers between devices: 226 us -> none  [on_device(): piece = lax.all_gather(arrived, ('ctx', 'ep'), axis=0, tiled=True)]
    all_to_all x0 -> x1, waiting for transfers between devices: none -> 102 us  [on_device(): all_to_all(jnp.stack([arrived for _ in range(axis_size(('ctx', 'ep')))],...]
  transfers between devices with their start and end apart: 8 -> 8, of which waited for: 7 -> 7; matrix products, arithmetic and copies ran while one was open for 21% -> 25% of each run, Pallas kernels for 0% -> 0%
where the time goes in v1:
time: 538 us; the launch traced here: 537 us
  waiting for transfers between devices  257 us (48%)
  matrix products  104 us (19%)
  blocking collectives  78.7 us (15%)
  local copies, waits for them, and re-layouts  54.2 us (10%)
  starting transfers between devices  23.7 us (4%)
  between operations  13.7 us (3%)
    all_to_all x1, waiting for transfers between devices, on_device(): all_to_all(jnp.stack([arrived for _ in range(axis_size(('ctx', 'ep')))],...  102 us
    reduce_scatter x1, waiting for transfers between devices, on_device(): lax.psum_scatter(product.reshape(blocks * capacity, tp_size * feat_dev).a...  88.1 us
    dot_general x16, matrix products, one_row(): jnp.einsum('tsj,tjf->sf', row, gate_part, preferred_element_type=jnp.floa...  43.6 us
    dot_general x16, matrix products, one_row(): jnp.einsum('tsj,tjf->sf', row, up_part, preferred_element_type=jnp.float32)  43.5 us
    all_gather x1, blocking collectives, on_device(): key_piece = lax.all_gather(keys, 'ctx', axis=0, tiled=True)  31.8 us
    all_gather x1, blocking collectives, on_device(): value_piece = lax.all_gather(values, 'ctx', axis=0, tiled=True)  30.6 us
    all_to_all x1, waiting for transfers between devices, sent_and_summed(): lax.all_to_all(tiles, axis, split_axis=0, concat_axis=0, tiled=True)  19.6 us
    all_gather x1, waiting for transfers between devices, on_device(): lax.all_gather(w_out, 'ctx', axis=1, tiled=True)  19.2 us
  transfers between devices with their start and end apart: 8, of which 7 were waited for; matrix products, arithmetic and copies ran while one was open for 25% of the time, Pallas kernels for 0%

profile of v1, /device:TPU:1, one launch (start us, length us, event | category | flops | bytes accessed | tf_op | source)
XLA Modules:
  0.0 536.5 jit_solution(15525446918843746384)
XLA Ops:
  9.4 31.8 %all_gather.9 = bf16[2048,128]{1,0:T(8,128)(2,1)S(1)} all-gather(bf16[256,128]{1,0:T(8,128)(2,1)} %param.15), channel_id=1, replica_groups=mesh['ctx'=8,'tp_0'=4,'tp_1'=2,'ep'=2] {'ctx'}, dimensions={0}, use_global_device_ids=true | all-gather | bytes 589824 | tf_op jit(solution)/shard_map/all_gather | solution.py:76
  43.6 30.6 %all_gather.10 = bf16[2048,128]{0,1:T(8,128)(2,1)S(1)} all-gather(bf16[256,128]{0,1:T(8,128)(2,1)S(1)} %copy.47), channel_id=1, replica_groups=mesh['ctx'=8,'tp_0'=4,'tp_1'=2,'ep'=2] {'ctx'}, dimensions={0}, use_global_device_ids=true | all-gather | bytes 589824 | tf_op jit(solution)/shard_map/all_gather | solution.py:77
  76.9 2.9 fusion.55
  79.8 19.2 %all-gather.2.cloned.1.call-done = bf16[768,3072]{1,0:T(8,128)(2,1)} async-done(((bf16[768,384]{1,0:T(8,128)(2,1)}), bf16[768,3072]{1,0:T(8,128)(2,1)}) %all-gather.2.cloned.1.call-update) | async-done | bytes 4718608 | tf_op jit(solution)/shard_map/all_gather | solution.py:99
  99.0 3.8 convolution_convert_fusion
  104.1 5.7 %all-to-all-start = ((bf16[8,256,384]{2,1,0:T(8,128)(2,1)}), bf16[8,256,384]{2,1,0:T(8,128)(2,1)S(1)}, u32[]{:S(2)}, u32[]{:S(2)}) async-start(bf16[8,256,384]{2,1,0:T(8,128)(2,1)} %bitcast.153), calls=%async_computation | async-start | bytes 3145728 | tf_op jit(solution)/shard_map/all_to_all | solution.py:22
  110.7 19.6 %all-to-all-done = bf16[8,256,384]{2,1,0:T(8,128)(2,1)S(1)} async-done(((bf16[8,256,384]{2,1,0:T(8,128)(2,1)}), bf16[8,256,384]{2,1,0:T(8,128)(2,1)S(1)}, u32[]{:S(2)}, u32[]{:S(2)}) %all-to-all-start) | async-done | bytes 1572896 | tf_op jit(solution)/shard_map/all_to_all | solution.py:22
  131.4 4.3 all-to-all-start.1
  135.7 5.9 %all-to-all-done.1 = f32[16,256,1]{1,2,0:T(1,128)S(1)} async-done(((f32[16,256,1]{1,2,0:T(1,128)}), f32[16,256,1]{1,2,0:T(1,128)S(1)}, u32[]{:S(2)}, u32[]{:S(2)}) %all-to-all-start.1) | async-done | bytes 16416 | tf_op jit(solution)/shard_map/all_to_all | solution.py:28
  142.1 4.2 all_to_all.40
  146.4 12.0 %all_to_all.41 = bf16[4,2,1,1,96,384]{5,4,1,3,2,0:T(8,128)(2,1)S(1)} all-to-all(bf16[4,2,1,1,96,384]{5,4,1,3,2,0:T(8,128)(2,1)S(1)} %copy.51), channel_id=1, replica_groups=mesh['ctx'=8,'tp_0'=4,'tp_1'=2,'ep'=2] {'tp_0'}, dimensions={0} | all-to-all | bytes 1179648 | tf_op jit(solution)/shard_map/all_to_all | solution.py:46
  158.4 4.9 stack.3
  163.3 5.3 all-to-all-start.4
  168.8 14.5 %reshape_squeeze.11 = bf16[512,8,2,384]{3,2,1,0:T(2,128)(2,1)} reshape(bf16[1,512,6144]{2,1,0:T(8,128)(2,1)} %param.21) | data formatting | bytes 12582912 | tf_op jit(solution)/shard_map/reshape;squeeze | solution.py:151
  183.4 15.4 %constant_dynamic-slice_fusion.3 = (bf16[512,8,1,384]{3,2,1,0:T(2,128)(2,1)}, bf16[512,8,1,384]{3,2,1,0:T(2,128)(2,1)S(1)}) fusion(bf16[512,8,2,384]{3,2,1,0:T(2,128)(2,1)} %reshape_squeeze.11, s32[]{:T(128)S(6)} %select_n.93, s32[]{:T(128)S(6)} %select_n.94), kind=kLoop, calls=%fused_computation.93 | loop fusion | bytes 12582920 | tf_op jit(solution)/shard_map/jit(dynamic_index_in_dim)/dynamic_slice | solution.py:153
  198.8 2.9 copy.71
  202.9 101.6 %all-to-all-done.4 = bf16[16,1,8,96,384]{4,3,2,1,0:T(8,128)(2,1)} async-done(((bf16[16,1,8,96,384]{4,3,2,1,0:T(8,128)(2,1)}), bf16[16,1,8,96,384]{4,3,2,1,0:T(8,128)(2,1)}, u32[]{:S(2)}, u32[]{:S(2)}) %all-to-all-start.4) | async-done | bytes 9437216 | tf_op jit(solution)/shard_map/all_to_all | solution.py:124
  305.0 88.4 %while.17 = (s32[]{:T(128)}, f32[8,96,512]{2,1,0:T(8,128)S(1)}, f32[8,96,512]{2,1,0:T(8,128)S(1)}, bf16[16,8,96,384]{3,2,1,0:T(8,128)(2,1)}, bf16[8,2,384,512]{3...) while((s32[]{:T(128)}, f32[8,96,512]{2,1,0:T(8,128)S(1)}, ...), condition=%wide.region_11.12_spmd, body=%wide.region_10.11_spmd.sunk | while | flops 604078080 | bytes 9045304 | solution.py:149
  305.0 2.7 fusion.102
  313.3 2.7 fusion.101
  316.1 2.7 fusion.102
  318.8 2.7 fusion.101
  321.6 2.7 fusion.102
  324.3 2.7 fusion.101
  329.8 2.7 fusion.101
  332.6 2.7 fusion.102
  335.4 2.7 fusion.101
  340.9 2.7 fusion.101
  343.7 2.7 fusion.102
  346.4 2.7 fusion.101
  351.9 2.7 fusion.101
  354.7 2.7 fusion.102
  357.5 2.7 fusion.101
  363.0 2.7 fusion.101
  365.8 2.7 fusion.102
  368.5 2.7 fusion.101
  374.0 2.7 fusion.101
  376.8 2.7 fusion.102
  379.6 2.7 fusion.101
  385.1 2.7 fusion.101
  390.6 2.7 fusion.101
  394.6 3.9 copy.72
  398.5 11.8 %collective-permute-done = bf16[8,96,512]{2,1,0:T(8,128)(2,1)S(1)} collective-permute-done((bf16[8,96,512]{2,1,0:T(8,128)(2,1)S(1)}, bf16[8,96,512]{2,1,0:T(8,128)(2,1)S(1)}, u32[]{:S(2)}, u32[]{:S(2)}) %collective-permute-start) | collective-permute-done | bytes 786464 | tf_op jit(solution)/shard_map/ppermute | solution.py:56
  410.3 6.7 %fusion.48 = bf16[8,96,8,384]{3,1,2,0:T(8,128)(2,1)S(1)} fusion(bf16[512,8,384]{2,0,1:T(8,128)(2,1)} %collective-permute-done.1, bf16[512,8,384]{2,0,1:T(8,128)(2,1)S(1)} %bitcast.179, bf16[8,96,512]{2,1,0:T(8,128)(2,1)S(1)} %collective-permute-done, bf16[8,96,512]{2,1,0:T(8,128)(2,1)S(1)} %multiply_convert_fusion), kind=kOutput, calls=%fused_computation.40 | convolution fusion | flops 4849926144 | bytes 12582912 | tf_op jit(solution)/shard_map/csf,ftj->cstj/dot_general | solution.py:159
  418.9 3.3 copy.66
  422.2 88.1 %reduce-scatter.2.cloned.1.call-done = bf16[96,3072]{1,0:T(8,128)(2,1)} async-done(((bf16[768,3072]{1,0:T(8,128)(2,1)}), bf16[96,3072]{1,0:T(8,128)(2,1)}) %reduce-scatter.2.cloned.1.call-update) | async-done | bytes 589840 | tf_op jit(solution)/shard_map/reduce_scatter | solution.py:162
  512.3 6.1 %all-to-all-start.5 = ((bf16[1,96,8,384]{3,1,0,2:T(8,128)(2,1)}), bf16[1,96,8,384]{3,1,0,2:T(8,128)(2,1)S(1)}, u32[]{:S(2)}, u32[]{:S(2)}) async-start(bf16[1,96,8,384]{3,1,0,2:T(8,128)(2,1)} %copy.57), calls=%async_computation.6 | async-start | bytes 1179648 | tf_op jit(solution)/shard_map/all_to_all | solution.py:169
  518.5 10.0 %all-to-all-done.5 = bf16[1,96,8,384]{3,1,0,2:T(8,128)(2,1)S(1)} async-done(((bf16[1,96,8,384]{3,1,0,2:T(8,128)(2,1)}), bf16[1,96,8,384]{3,1,0,2:T(8,128)(2,1)S(1)}, u32[]{:S(2)}, u32[]{:S(2)}) %all-to-all-start.5) | async-done | bytes 589856 | tf_op jit(solution)/shard_map/all_to_all | solution.py:169
  (80 shorter events, 45.1 us)
Async XLA Ops:
  6.5 92.4 %all-gather.2.cloned.1.call-start = ((), (), s32[]{:S(2)}) async-start(), calls=%async_computation.7 | async-start | bytes 5308416 | tf_op jit(solution)/shard_map/all_gather | solution.py:99
  102.7 7.1 %copy-start.3 = (s32[256,2]{0,1:T(2,128)S(1)}, s32[256,2]{0,1:T(2,128)}, u32[]{:S(2)}) copy-start(s32[256,2]{0,1:T(2,128)} %param.22) | copy-start | bytes 6148
  102.7 27.8 %copy-start = (bf16[256,384]{1,0:T(8,128)(2,1)S(1)}, bf16[256,384]{1,0:T(8,128)(2,1)}, u32[]{:S(2)}) copy-start(bf16[256,384]{1,0:T(8,128)(2,1)} %param.13) | copy-start | bytes 589828
  102.7 32.9 %copy-start.5 = (bf16[384]{0:T(512)(128)(2,1)S(1)}, bf16[384]{0:T(512)(128)(2,1)}, u32[]{:S(2)}) copy-start(bf16[384]{0:T(512)(128)(2,1)} %param.18) | copy-start | bytes 2308
  104.1 26.3 %all-to-all-start = ((bf16[8,256,384]{2,1,0:T(8,128)(2,1)}), bf16[8,256,384]{2,1,0:T(8,128)(2,1)S(1)}, u32[]{:S(2)}, u32[]{:S(2)}) async-start(bf16[8,256,384]{2,1,0:T(8,128)(2,1)} %bitcast.153), calls=%async_computation | async-start | bytes 3145728 | tf_op jit(solution)/shard_map/all_to_all | solution.py:22
  130.7 32.6 %copy-start.1 = (bf16[256,384]{1,0:T(8,128)(2,1)}, bf16[256,384]{1,0:T(8,128)(2,1)S(1)}, u32[]{:S(2)}) copy-start(bf16[256,384]{1,0:T(8,128)(2,1)S(1)} %get-tuple-element.198) | copy-start | bytes 589828
  131.4 10.2 %all-to-all-start.1 = ((f32[16,256,1]{1,2,0:T(1,128)}), f32[16,256,1]{1,2,0:T(1,128)S(1)}, u32[]{:S(2)}, u32[]{:S(2)}) async-start(f32[16,256,1]{1,2,0:T(1,128)} %broadcast_in_dim.96), calls=%async_computation.1 | async-start | bytes 32768 | tf_op jit(solution)/shard_map/all_to_all | solution.py:28
  163.3 141.2 %all-to-all-start.4 = ((bf16[16,1,8,96,384]{4,3,2,1,0:T(8,128)(2,1)}), bf16[16,1,8,96,384]{4,3,2,1,0:T(8,128)(2,1)}, u32[]{:S(2)}, u32[]{:S(2)}) async-start(bf16[16,1,8,96,384]{4,3,2,1,0:T(8,128)(2,1)} %stack.3), calls=%async_computation.4 | async-start | bytes 18874368 | tf_op jit(solution)/shard_map/all_to_all | solution.py:124
  168.6 341.7 %reduce-scatter.2.cloned.1.call-start = ((), (), s32[]{:S(2)}) async-start(), calls=%async_computation.8 | async-start | bytes 5308416 | tf_op jit(solution)/shard_map/reduce_scatter | solution.py:162
  201.6 196.9 %collective-permute-start.1 = (bf16[512,8,384]{2,0,1:T(8,128)(2,1)}, bf16[512,8,384]{2,0,1:T(8,128)(2,1)}, u32[]{:S(2)}, u32[]{:S(2)}) collective-permute-start(bf16[512,8,384]{2,0,1:T(8,128)(2,1)} %bitcast.150), channel_id=1, source_target_pairs={{0,1},{1,0},{2,3},{3,2},{4,5},{5,4},{6,7},{7,6},{8,9},{9,8},{10,11... | collective-permute-start | bytes 9437192 | tf_op jit(solution)/shard_map/ppermute | solution.py:56
  393.8 16.5 %collective-permute-start = (bf16[8,96,512]{2,1,0:T(8,128)(2,1)S(1)}, bf16[8,96,512]{2,1,0:T(8,128)(2,1)S(1)}, u32[]{:S(2)}, u32[]{:S(2)}) collective-permute-start(bf16[8,96,512]{2,1,0:T(8,128)(2,1)S(1)} %multiply_convert_fusion), channel_id=1, source_target_pairs={{0,1},{1,0},{2,3},{3,2},{4,5},{5,4},{6,7},{7,6},{8,9},{9,8},{10,11... | collective-permute-start | bytes 2359304 | tf_op jit(solution)/shard_map/ppermute | solution.py:56
  422.2 96.2 %copy-start.4 = (s32[256,2]{0,1:T(2,128)S(1)}, s32[256,2]{0,1:T(2,128)}, u32[]{:S(2)}) copy-start(s32[256,2]{0,1:T(2,128)} %param.23) | copy-start | bytes 6148
  422.2 106.3 %copy-start.2 = (bf16[256,384]{1,0:T(8,128)(2,1)S(1)}, bf16[256,384]{1,0:T(8,128)(2,1)}, u32[]{:S(2)}) copy-start(bf16[256,384]{1,0:T(8,128)(2,1)} %copy-done.1) | copy-start | bytes 589828
  512.3 16.2 %all-to-all-start.5 = ((bf16[1,96,8,384]{3,1,0,2:T(8,128)(2,1)}), bf16[1,96,8,384]{3,1,0,2:T(8,128)(2,1)S(1)}, u32[]{:S(2)}, u32[]{:S(2)}) async-start(bf16[1,96,8,384]{3,1,0,2:T(8,128)(2,1)} %copy.57), calls=%async_computation.6 | async-start | bytes 1179648 | tf_op jit(solution)/shard_map/all_to_all | solution.py:169
Sparse Core Ops, SparseCore 0:
  9.5 89.3 all-gather.1
  422.3 87.8 reduce-scatter.1
